TPU v7x, 32 devices: a whole 2x2x4 slice. The times are simulated.
32 devices in a mesh: groups: 2 (over y), expert: 8 (over z, core), tensor: 2 (over x).
Axes of the slice: x: 2, y: 2, z: 4, core: 2. Of those that a mesh axis runs over, the one named last changes fastest.
Arguments:
- hidden_in: bfloat16 [128, 2880], P(('groups', 'expert')), parts along dimension 0, may hold values from -6 to 6
- queries: bfloat16 [128, 32, 64], P(('groups', 'expert'), 'tensor'), parts along dimension 0, may hold values from -8 to 8
- new_keys: bfloat16 [128, 8, 64], P(('groups', 'expert'), 'tensor'), parts along dimension 0, may hold values from -4 to 4
- new_values: bfloat16 [128, 8, 64], P(('groups', 'expert'), 'tensor'), parts along dimension 0, may hold values from -4 to 4
- cache_keys: bfloat16 [128, 8, 64, 256], P(('groups', 'expert'), 'tensor'), parts along dimension 0, may hold values from -8 to 8
- cache_values: bfloat16 [128, 8, 64, 256], P(('groups', 'expert'), 'tensor'), parts along dimension 0, may hold values from -4 to 4
- cache_lengths: int32 [128], P(('groups', 'expert')), parts along dimension 0, may hold values from 2 to 256, as said below
- out_weight: bfloat16 [2048, 2880], P('tensor'), may hold values from -0.125 to 0.125
- norm_gain: float32 [2880], replicated, may hold values from 0.1 to 1.9
- expert_ids: int32 [128, 4], P(('groups', 'expert')), parts along dimension 0, may hold values from 0 to 7, all different within a row; in each aligned block of 8 rows (0 to 7, 8 to 15, ...) at most 4 rows name the same one
- route_probs: float32 [128, 4], P(('groups', 'expert')), parts along dimension 0, may hold values from 0.05 to 1
- route_order: int32 [128, 4], P(('groups', 'expert')), parts along dimension 0, may hold values from 0 to 3, each once within a row
- gate_weight: bfloat16 [8, 2880, 1440], P('expert', None, 'tensor'), may hold values from -0.109375 to 0.109375
- up_weight: bfloat16 [8, 2880, 1440], P('expert', None, 'tensor'), may hold values from -0.109375 to 0.109375
- down_weight: bfloat16 [8, 1440, 2880], P('expert', 'tensor'), may hold values from -0.15625 to 0.15625
Outputs:
- layer_out: bfloat16 [128, 2880], P(('groups', 'expert'), 'tensor'), parts along dimension 0
There are 2 independent parts, one for each index of `groups`. A program takes and returns all parts, laid end to end along the dimension named above; an argument that names none is the same for every part. Nothing has to cross between parts.
Inputs may be any that keep to these rules, and one draw needn't show every extreme that they name: `cache_lengths`: some sequence fills all 256 slots. `expert_ids`: each row names 4 different experts; among the 8 rows of one device no expert is named by more than 4 rows, a bound that some block reaches. `route_order`: each row is a permutation of 0 to 3.
All inputs are finite; a program needn't handle non-finite values.
Results may differ from a plain program's by a relative error of at most 0.007.
Values may be sent and summed in bfloat16 or wider, within the bound.
A program may use at most 64 MiB of HBM per device.

v0:
```python
import jax
import jax.numpy as jnp
from jax import lax
from jax.sharding import PartitionSpec as P

EPSILON = 1e-05
GLU_SLOPE = 1.702


def attend(queries, new_keys, new_values, cache_keys, cache_values, cache_lengths):
    sequence_count, head_count, head_dim = queries.shape
    kv_heads = new_keys.shape[1]
    group_size = head_count // kv_heads
    scaling = 1.0 / head_dim**0.5
    query_rows = queries.reshape(sequence_count, kv_heads, group_size, head_dim)
    scores = (
        jnp.einsum("sgqd,sgdc->sgqc", query_rows, cache_keys, preferred_element_type=jnp.float32)
        * scaling
    )
    own_score = (
        jnp.einsum("sgqd,sgd->sgq", query_rows, new_keys, preferred_element_type=jnp.float32)
        * scaling
    )
    positions = jnp.arange(cache_keys.shape[3], dtype=jnp.int32)
    visible = positions[None, :] < cache_lengths[:, None]
    scores = jnp.where(visible[:, None, None, :], scores, -1e30)
    highest = jnp.maximum(jnp.max(scores, axis=3), own_score)
    cache_exp = jnp.exp(scores - highest[..., None])
    own_exp = jnp.exp(own_score - highest)
    totals = jnp.sum(cache_exp, axis=3) + own_exp
    cache_prob = (cache_exp / totals[..., None]).astype(jnp.bfloat16)
    own_prob = (own_exp / totals).astype(jnp.bfloat16)
    attended = jnp.einsum(
        "sgqc,sgdc->sgqd", cache_prob, cache_values, preferred_element_type=jnp.float32
    )
    attended = (
        attended
        + own_prob.astype(jnp.float32)[..., None] * new_values.astype(jnp.float32)[:, :, None, :]
    )
    return attended.astype(jnp.bfloat16).reshape(sequence_count, head_count * head_dim)


def apply_norm(residual, norm_gain):
    mean_square = jnp.mean(residual * residual, axis=1, keepdims=True)
    return (residual * lax.rsqrt(mean_square + EPSILON) * norm_gain).astype(jnp.bfloat16)


def route_tables(expert_ids, route_probs, route_order, experts, capacity):
    tokens, top_count = expert_ids.shape
    flat_ids = expert_ids.reshape(tokens * top_count)
    expert_mark = (flat_ids[:, None] == jnp.arange(experts, dtype=jnp.int32)[None, :]).astype(
        jnp.int32
    )
    earlier = jnp.cumsum(expert_mark, axis=0) - expert_mark
    position = jnp.sum(earlier * expert_mark, axis=1)
    slot_code = flat_ids * capacity + position
    slot_table = slot_code[:, None] == jnp.arange(experts * capacity, dtype=jnp.int32)[None, :]
    slot_table = slot_table.astype(jnp.float32).reshape(tokens, top_count, experts * capacity)
    picked = jnp.zeros((tokens, top_count), jnp.float32)
    for column in range(top_count):
        picked = picked + jnp.where(route_order == column, route_probs[:, column : column + 1], 0.0)
    weights = picked / jnp.sum(route_probs, axis=1, keepdims=True)
    select_experts = jnp.sum(slot_table, axis=1)
    weighted_output = jnp.sum(slot_table * weights[:, :, None], axis=1)
    return (select_experts, weighted_output)


def per_device(
    hidden_in,
    queries,
    new_keys,
    new_values,
    cache_keys,
    cache_values,
    cache_lengths,
    out_weight,
    norm_gain,
    expert_ids,
    route_probs,
    route_order,
    gate_weight,
    up_weight,
    down_weight,
):
    sequence_count, model_width = hidden_in.shape
    expert_ranks = lax.axis_size("expert")
    tensor_ranks = lax.axis_size("tensor")
    local_experts = gate_weight.shape[0]
    experts = local_experts * expert_ranks
    top_count = expert_ids.shape[1]
    capacity = min(sequence_count, max(2, (sequence_count * top_count + experts - 1) // experts))
    slab_width = model_width // tensor_ranks
    offset = lax.axis_index("tensor") * slab_width
    attended = attend(queries, new_keys, new_values, cache_keys, cache_values, cache_lengths)
    partial_sums = jnp.dot(attended, out_weight, preferred_element_type=jnp.float32)
    attention = lax.psum(partial_sums, "tensor")
    residual = hidden_in.astype(jnp.float32) + attention
    normed = apply_norm(residual, norm_gain)
    select_experts, weighted_output = route_tables(
        expert_ids, route_probs, route_order, experts, capacity
    )
    outgoing = jnp.dot(
        select_experts.T.astype(jnp.bfloat16), normed, preferred_element_type=jnp.float32
    ).astype(jnp.bfloat16)
    outgoing = outgoing.reshape(expert_ranks, local_experts * capacity, model_width)
    arrived = lax.all_to_all(outgoing, "expert", split_axis=0, concat_axis=0, tiled=True)
    arrived = arrived.reshape(expert_ranks, local_experts, capacity, model_width)
    gate_sums = jnp.einsum(
        "secd,edf->secf", arrived, gate_weight, preferred_element_type=jnp.float32
    )
    upward = jnp.einsum("secd,edf->secf", arrived, up_weight, preferred_element_type=jnp.float32)
    active = (gate_sums * jax.nn.sigmoid(GLU_SLOPE * gate_sums) * (upward + 1.0)).astype(
        jnp.bfloat16
    )
    expert_part = jnp.einsum(
        "secf,efd->secd", active, down_weight, preferred_element_type=jnp.float32
    )
    expert_part = expert_part.reshape(expert_ranks, local_experts * capacity, model_width)
    kept = lax.dynamic_slice_in_dim(residual, offset, slab_width, 1)
    returned = lax.all_to_all(expert_part, "expert", split_axis=0, concat_axis=0, tiled=True)
    returned = returned.reshape(experts * capacity, model_width)
    blended = jnp.dot(weighted_output, returned, precision=lax.Precision.HIGHEST)
    expert_mixture = lax.psum_scatter(
        blended.astype(jnp.bfloat16), "tensor", scatter_dimension=1, tiled=True
    ).astype(jnp.float32)
    return (kept + expert_mixture).astype(jnp.bfloat16)


def solution(mesh):
    in_specs = (
        P(("groups", "expert"), None),
        P(("groups", "expert"), "tensor", None),
        P(("groups", "expert"), "tensor", None),
        P(("groups", "expert"), "tensor", None),
        P(("groups", "expert"), "tensor", None, None),
        P(("groups", "expert"), "tensor", None, None),
        P(("groups", "expert")),
        P("tensor", None),
        P(),
        P(("groups", "expert"), None),
        P(("groups", "expert"), None),
        P(("groups", "expert"), None),
        P("expert", None, "tensor"),
        P("expert", None, "tensor"),
        P("expert", "tensor", None),
    )
    out_specs = P(("groups", "expert"), "tensor")
    return jax.shard_map(
        per_device, mesh=mesh, in_specs=in_specs, out_specs=out_specs, check_vma=False
    )
```

profile of v0, /device:TPU:0, one launch (start us, length us, event | category | flops | bytes accessed | tf_op | source)
XLA Modules:
  0.0 103.0 jit_solution(494024333283374364)
XLA Ops:
  6.5 0.0 copy-start
  6.5 0.0 all-reduce.2.cloned.1.call-start
  6.5 0.8 iota_compare_fusion.2
  7.4 0.9 fusion.35
  8.3 0.0 copy-done
  8.3 1.1 %fusion.40 = (f32[8,4,4]{2,1,0:T(4,128)S(1)}, f32[8,4,4,256]{3,2,1,0:T(4,128)S(1)}) fusion(bf16[8,4,4,64]{3,2,1,0:T(4,128)(2,1)} %bitcast.74, bf16[8,4,64,256]{3,2,1,0:T(8,128)(2,1)S(1)} %copy-done, pred[8,256]{1,0:T(8,128)(4,1)S(1)} %iota_compare_fusion.2), kind=kOutput, calls=%fused_computation.54 | convolution fusion | flops 4292480 | bytes 1198592 | tf_op jit(solution)/shard_map/sgqd,sgdc->sgqc/dot_general | solution.py:17
  9.4 0.0 copy-start.3
  9.4 0.0 copy-start.4
  9.4 0.2 fusion.28
  9.6 0.0 copy-start.5
  9.6 0.0 copy-start.1
  9.7 0.7 convert_element_type.51
  10.4 0.0 copy-start.2
  10.4 1.7 %fusion.22 = bf16[8,4,4,64]{3,2,1,0:T(4,128)(2,1)S(1)} fusion(bf16[8,4,64,256]{3,2,1,0:T(8,128)(2,1)} %param.20, f32[8,4,4,256]{3,2,1,0:T(4,128)S(1)} %get-tuple-element.16, f32[8,4,4]{2,1,0:T(4,128)S(1)} %get-tuple-element.10, f32[8,4,4]{2,1,0:T(4,128)S(1)} %multiply_maximum_fusion, f32[8,4,64]{2,1,0:T(4,128)S(1)} %convert_element_type.51, ...), kind=kOutput, calls=%fused_computation.16 | convolution fusion | flops 4317184 | bytes 1205760 | tf_op jit(solution)/shard_map/sgqc,sgdc->sgqd/dot_general | solution.py:33
  12.1 0.1 reshape.87
  12.2 5.0 %fusion.41 = f32[8,2880]{1,0:T(8,128)} fusion(bf16[8,1024]{1,0:T(8,128)(2,1)S(1)} %reshape.87, bf16[1024,2880]{0,1:T(8,128)(2,1)} %param.22), kind=kOutput, calls=%fused_computation.55 | convolution fusion | flops 47185920 | bytes 6006784 | tf_op jit(solution)/shard_map/dot_general | solution.py:95
  17.2 0.0 all-reduce.2.cloned.1.call-update
  17.2 0.0 reduce-scatter.4.cloned.1.call-start
  17.2 0.0 copy-done.3
  17.3 0.0 copy-done.4
  17.3 0.1 copy.31
  17.4 0.1 eq.53
  17.4 0.1 fusion.34
  17.5 0.1 reduce_window_sum.11
  17.6 0.2 select_reduce_fusion.1
  17.8 0.1 reduce_sum.58
  17.8 0.1 copy.33
  17.9 0.0 copy-done.5
  18.0 0.1 convert_reduce_fusion
  18.0 23.1 %all-reduce.2.cloned.1.call-done = f32[8,2880]{1,0:T(8,128)} async-done(((f32[8,2880]{1,0:T(8,128)}), f32[8,2880]{1,0:T(8,128)}) %all-reduce.2.cloned.1.call-update) | async-done | bytes 92176 | tf_op jit(solution)/shard_map/psum | solution.py:96
  41.2 0.0 copy-done.1
  41.2 1.0 %multiply_reduce_fusion = (f32[8]{0:T(128)S(1)}, f32[8,2880]{1,0:T(8,128)S(1)}) fusion(f32[8,2880]{1,0:T(8,128)} %all-reduce.2.cloned.1.call-done, bf16[8,2880]{1,0:T(8,128)(2,1)S(1)} %copy-done.1), kind=kLoop, calls=%fused_computation.24 | loop fusion | flops 92152 | bytes 230432 | tf_op jit(solution)/shard_map/reduce_sum | solution.py:44
  42.2 0.0 copy-done.2
  42.2 0.3 convolution_convert_fusion
  42.5 0.1 reshape.88
  42.6 12.5 %all_to_all.10 = bf16[8,4,2880]{2,1,0:T(4,128)(2,1)S(1)} all-to-all(bf16[8,4,2880]{2,1,0:T(4,128)(2,1)S(1)} %reshape.88), channel_id=1, replica_groups=mesh['groups'=2,'expert'=8,'tensor'=2] {'expert'}, dimensions={0} | all-to-all | bytes 368640 | tf_op jit(solution)/shard_map/all_to_all | solution.py:106
  55.1 0.0 slice-start
  55.1 3.6 %fusion.7 = f32[8,1,4,720]{3,0,2,1:T(8,128)S(1)} fusion(bf16[1,2880,720]{1,2,0:T(8,128)(2,1)} %param.27, bf16[8,4,2880]{2,1,0:T(4,128)(2,1)S(1)} %all_to_all.10), kind=kOutput, calls=%fused_computation.10 | convolution fusion | flops 132710400 | bytes 4423680 | tf_op jit(solution)/shard_map/secd,edf->secf/dot_general | solution.py:108
  58.8 0.0 slice-start.1
  58.8 3.5 %fusion.23 = bf16[8,4,720]{2,0,1:T(8,128)(2,1)S(1)} fusion(bf16[1,2880,720]{1,2,0:T(8,128)(2,1)} %param.28, bf16[8,4,2880]{2,1,0:T(4,128)(2,1)S(1)} %all_to_all.10, f32[8,1,4,720]{3,0,2,1:T(8,128)S(1)} %fusion.7), kind=kOutput, calls=%fused_computation.17 | convolution fusion | flops 132894720 | bytes 4469760 | tf_op jit(solution)/shard_map/secd,edf->secf/dot_general | solution.py:111
  62.3 0.0 slice-done
  62.3 0.0 slice-done.1
  62.3 0.8 fusion
  63.1 14.5 %all_to_all.11 = f32[8,4,2880]{2,1,0:T(4,128)S(1)} all-to-all(f32[8,4,2880]{2,1,0:T(4,128)S(1)} %fusion), channel_id=1, replica_groups=mesh['groups'=2,'expert'=8,'tensor'=2] {'expert'}, dimensions={0} | all-to-all | bytes 737280 | tf_op jit(solution)/shard_map/all_to_all | solution.py:120
  77.7 0.1 reshape.93
  77.8 0.3 convolution_convert_fusion.1
  78.1 1.2 %copy.41 = bf16[8,2880]{0,1:T(8,128)(2,1)} copy(bf16[8,2880]{1,0:T(8,128)(2,1)S(1)} %convolution_convert_fusion.1) | data formatting | bytes 92160
  79.2 0.0 reduce-scatter.4.cloned.1.call-update
  79.3 15.1 %reduce-scatter.4.cloned.1.call-done = bf16[1440,8]{1,0:T(8,128)(2,1)} async-done(((bf16[2880,8]{1,0:T(8,128)(2,1)}), bf16[1440,8]{1,0:T(8,128)(2,1)}) %reduce-scatter.4.cloned.1.call-update) | async-done | bytes 23056
  94.4 1.1 %copy.42 = bf16[8,1440]{1,0:T(8,128)(2,1)S(1)} copy(bf16[8,1440]{0,1:T(8,128)(2,1)} %bitcast.70) | data formatting | bytes 46080
  95.5 0.7 add_convert_fusion
  (8 shorter events, 0.1 us)
Async XLA Ops:
  6.5 1.7 %copy-start = (bf16[8,4,64,256]{3,2,1,0:T(8,128)(2,1)S(1)}, bf16[8,4,64,256]{3,2,1,0:T(8,128)(2,1)}, u32[]{:S(2)}) copy-start(bf16[8,4,64,256]{3,2,1,0:T(8,128)(2,1)} %param.19) | copy-start | bytes 3145732
  6.5 34.6 %all-reduce.2.cloned.1.call-start = ((), (), s32[]{:S(2)}) async-start(), calls=%async_computation.3 | async-start | bytes 188416 | tf_op jit(solution)/shard_map/psum | solution.py:96
  9.4 7.8 %copy-start.3 = (f32[8,4]{0,1:T(4,128)S(1)}, f32[8,4]{0,1:T(4,128)}, u32[]{:S(2)}) copy-start(f32[8,4]{0,1:T(4,128)} %param.25) | copy-start | bytes 388
  9.4 7.9 %copy-start.4 = (s32[8,4]{0,1:T(4,128)S(1)}, s32[8,4]{0,1:T(4,128)}, u32[]{:S(2)}) copy-start(s32[8,4]{0,1:T(4,128)} %param.24) | copy-start | bytes 388
  9.6 8.3 %copy-start.5 = (s32[8,4]{0,1:T(4,128)S(1)}, s32[8,4]{0,1:T(4,128)}, u32[]{:S(2)}) copy-start(s32[8,4]{0,1:T(4,128)} %param.26) | copy-start | bytes 388
  9.6 31.5 %copy-start.1 = (bf16[8,2880]{1,0:T(8,128)(2,1)S(1)}, bf16[8,2880]{1,0:T(8,128)(2,1)}, u32[]{:S(2)}) copy-start(bf16[8,2880]{1,0:T(8,128)(2,1)} %param.15) | copy-start | bytes 138244
  10.4 31.8 %copy-start.2 = (f32[2880]{0:T(1024)S(1)}, f32[2880]{0:T(1024)}, u32[]{:S(2)}) copy-start(f32[2880]{0:T(1024)} %param.23) | copy-start | bytes 34564
  17.2 77.2 %reduce-scatter.4.cloned.1.call-start = ((), (), s32[]{:S(2)}) async-start(), calls=%async_computation.4 | async-start | bytes 1105920
  55.1 7.2 %slice-start = ((s8[4239360]{0:T(1024)(128)(4,1)}), s8[4194304]{0:T(1024)(128)(4,1)S(1)}, s32[]{:S(2)}) async-start(s8[4239360]{0:T(1024)(128)(4,1)} %bitcast.67), calls=%async_computation.5 | async-start | bytes 8388608
  58.8 3.5 %slice-start.1 = ((s8[4239360]{0:T(1024)(128)(4,1)}), s8[45056]{0:T(1024)(128)(4,1)S(1)}, s32[]{:S(2)}) async-start(s8[4239360]{0:T(1024)(128)(4,1)} %bitcast.67), calls=%async_computation.6 | async-start | bytes 90112
Sparse Core Ops, SparseCore 0:
  17.3 23.8 all-reduce.1
  79.4 14.9 reduce-scatter.3
where the time goes:
time: 104 us; the launch traced here: 103 us
  waiting for transfers between devices  38.3 us (37%)
  blocking collectives  27.1 us (26%)
  matrix products  17.2 us (17%)
  between operations  13.6 us (13%)
  other arithmetic  3.95 us (4%)
  local copies, waits for them, and re-layouts  2.93 us (3%)
    psum x1, waiting for transfers between devices, per_device(): attention = lax.psum(partial_sums, 'tensor')  23.1 us
    unnamed x3, waiting for transfers between devices  15.1 us
    all_to_all x1, blocking collectives, per_device(): lax.all_to_all(expert_part, 'expert', split_axis=0, concat_axis=0, tiled=...  14.5 us
    all_to_all x1, blocking collectives, per_device(): lax.all_to_all(outgoing, 'expert', split_axis=0, concat_axis=0, tiled=True)  12.5 us
    dot_general x1, matrix products, per_device(): jnp.dot(attended, out_weight, preferred_element_type=jnp.float32)  4.97 us
    dot_general x1, matrix products, per_device(): jnp.einsum('secd,edf->secf', arrived, gate_weight, preferred_element_type...  3.63 us
    dot_general x1, matrix products, per_device(): jnp.einsum('secd,edf->secf', arrived, up_weight, preferred_element_type=j...  3.5 us
    unnamed x19, local copies, waits for them, and re-layouts  2.39 us
  transfers between devices with their start and end apart: 2, of which 2 were waited for; matrix products, arithmetic and copies ran while one was open for 1% of the time, Pallas kernels for 0%

commit v1 on v0

v1 whole, which is shorter than its diff:
```python
import functools

import jax
import jax.numpy as jnp
from jax import lax
from jax.experimental import pallas as pl
from jax.experimental.pallas import tpu as pltpu
from jax.sharding import PartitionSpec as P

EPSILON = 1e-05
GLU_SLOPE = 1.702
MESH = pl.DeviceIdType.MESH
BF16 = jnp.bfloat16
F32 = jnp.float32
CHUNK = 1024


def dot(a, b):
    return jnp.dot(a, b, preferred_element_type=F32)


def dot_nt(a, b):
    return lax.dot_general(a, b, (((1,), (1,)), ((), ())), preferred_element_type=F32)


def dot_tn(a, b):
    return lax.dot_general(a, b, (((0,), (0,)), ((), ())), preferred_element_type=F32)


def widths_of(total):
    out = []
    start = 0
    while start < total:
        out.append((start, min(CHUNK, total - start)))
        start += CHUNK
    return out


def kernel(
    sizes,
    len_ref,
    hid_ref,
    q_ref,
    nk_ref,
    nv_ref,
    gain_ref,
    ids_ref,
    probs_ref,
    order_ref,
    k_hbm,
    v_hbm,
    w_hbm,
    gate_hbm,
    up_hbm,
    down_hbm,
    out_ref,
    kbuf,
    vbuf,
    wbuf,
    gbuf,
    ubuf,
    dbuf,
    res_slab,
    disp_send,
    disp_recv,
    part_send,
    part_recv,
    ret_send,
    ret_recv,
    local_sem,
    xs_sem,
    xr_sem,
    ds_sem,
    dr_sem,
    ps_sem,
    pr_sem,
    rs_sem,
    rr_sem,
    *x_bufs,
):
    S, H, G, HD, C, D, F, E, T, cap = sizes
    R = H // G
    slab = D // T
    chunks = widths_of(D)
    x_send, x_recv = x_bufs[: len(chunks)], x_bufs[len(chunks) :]
    me_e = lax.axis_index("expert")
    me_t = lax.axis_index("tensor")

    copies = []
    for n, (src, dst) in enumerate(
        (
            (k_hbm, kbuf),
            (v_hbm, vbuf),
            (w_hbm, wbuf),
            (gate_hbm.at[0], gbuf),
            (up_hbm.at[0], ubuf),
            (down_hbm.at[0], dbuf),
        )
    ):
        copies.append(pltpu.make_async_copy(src, dst, local_sem.at[n]))
    for copy in copies:
        copy.start()

    barrier = pltpu.get_barrier_semaphore()
    tensor_peers = [lax.rem(me_t + i, T) for i in range(1, T)]
    expert_peers = [lax.rem(me_e + i, E) for i in range(1, E)]
    for peer in tensor_peers:
        pl.semaphore_signal(barrier, inc=1, device_id={"tensor": peer}, device_id_type=MESH)
    for peer in expert_peers:
        pl.semaphore_signal(barrier, inc=1, device_id={"expert": peer}, device_id_type=MESH)

    ids = ids_ref[...]
    probs = probs_ref[...]
    order = order_ref[...]
    top = ids.shape[0]
    slots = E * cap
    row = lax.broadcasted_iota(jnp.int32, (slots, S), 0)
    slot_expert = row // cap
    slot_place = (row % cap).astype(F32)
    picked = jnp.zeros((top, S), F32)
    for j in range(top):
        picked = picked + jnp.where(order == j, probs[j : j + 1], 0.0)
    weights = picked / jnp.sum(probs, axis=0, keepdims=True)
    member = jnp.zeros((slots, S), F32)
    mixture = jnp.zeros((slots, S), F32)
    for j in range(top):
        hit = ids[j : j + 1] == slot_expert
        member = member + jnp.where(hit, 1.0, 0.0)
        mixture = mixture + jnp.where(hit, weights[j : j + 1], 0.0)
    earlier = jnp.where(
        lax.broadcasted_iota(jnp.int32, (S, S), 0) < lax.broadcasted_iota(jnp.int32, (S, S), 1),
        1.0,
        0.0,
    )
    place = dot(member.astype(BF16), earlier.astype(BF16))
    sel = jnp.where(place == slot_place, member, 0.0)
    mixture = mixture * sel
    mix_hi = mixture.astype(BF16)
    rest = mixture - mix_hi.astype(F32)
    mix_mid = rest.astype(BF16)
    mix_lo = (rest - mix_mid.astype(F32)).astype(BF16)

    scaling = 1.0 / HD**0.5
    width = G * HD
    diagonal = (lax.broadcasted_iota(jnp.int32, (H, width), 0) // R) == (
        lax.broadcasted_iota(jnp.int32, (H, width), 1) // HD
    )
    position = lax.broadcasted_iota(jnp.int32, (H, C), 1)
    copies[0].wait()
    scores, owns = [], []
    for s in range(S):
        wide = jnp.concatenate([q_ref[s].astype(F32)] * G, axis=1)
        wide = jnp.where(diagonal, wide, 0.0)
        raw = dot(wide.astype(BF16), kbuf[s].reshape(width, C)) * scaling
        scores.append(jnp.where(position < len_ref[s], raw, -1e30))
        new_key = nk_ref[s].astype(F32)
        row = jnp.concatenate([new_key[g : g + 1] for g in range(G)], axis=1)
        owns.append(jnp.sum(wide * row, axis=1, keepdims=True) * scaling)
    score = jnp.concatenate(scores, axis=0)
    own = jnp.concatenate(owns, axis=0)
    highest = jnp.maximum(jnp.max(score, axis=1, keepdims=True), own)
    grown = jnp.exp(score - highest)
    own_grown = jnp.exp(own - highest)
    total = jnp.sum(grown, axis=1, keepdims=True) + own_grown
    prob = (grown / total).astype(BF16)
    own_prob = (own_grown / total).astype(BF16).astype(F32)
    copies[1].wait()
    attended = []
    for s in range(S):
        rows = slice(s * H, (s + 1) * H)
        mixed = dot_nt(prob[rows], vbuf[s].reshape(width, C))
        new_value = nv_ref[s].astype(F32)
        row = jnp.concatenate([new_value[g : g + 1] for g in range(G)], axis=1)
        attended.append(jnp.where(diagonal, mixed + own_prob[rows] * row, 0.0))
    attended = jnp.concatenate(attended, axis=0).astype(BF16)
    out_row = lax.broadcasted_iota(jnp.int32, (R * S, S * H), 0)
    in_row = lax.broadcasted_iota(jnp.int32, (R * S, S * H), 1)
    regroup = jnp.where(
        ((out_row % S) == (in_row // H)) & ((out_row // S) == (in_row % R)), 1.0, 0.0
    ).astype(BF16)
    grouped = dot(regroup, attended)
    heads = jnp.concatenate(
        [
            grouped[r * S : (r + 1) * S, g * HD : (g + 1) * HD]
            for g in range(G)
            for r in range(R)
        ],
        axis=1,
    ).astype(BF16)

    pl.semaphore_wait(barrier, (T - 1) + (E - 1))
    copies[2].wait()
    partials, x_copies = [], []
    for c, (start, size) in enumerate(chunks):
        partial = dot_nt(heads, wbuf[start : start + size])
        partials.append(partial)
        x_send[c][...] = partial.astype(BF16)
        for i, peer in enumerate(tensor_peers):
            copy = pltpu.make_async_remote_copy(
                src_ref=x_send[c],
                dst_ref=x_recv[c].at[i],
                send_sem=xs_sem.at[c, i],
                recv_sem=xr_sem.at[c, i],
                device_id={"tensor": peer},
                device_id_type=MESH,
            )
            copy.start()
            x_copies.append((c, i, copy))
    residuals = [hid_ref[:, a : a + n].astype(F32) + partials[c] for c, (a, n) in enumerate(chunks)]
    for c, i, copy in x_copies:
        copy.wait()
        residuals[c] = residuals[c] + x_recv[c][i].astype(F32)
    residual = jnp.concatenate(residuals, axis=1)
    mean_square = jnp.sum(residual * residual, axis=1, keepdims=True) * (1.0 / D)
    normed = (residual * lax.rsqrt(mean_square + EPSILON) * gain_ref[...].reshape(1, D)).astype(BF16)
    for t in range(T):
        res_slab[t] = residual[:, t * slab : (t + 1) * slab]

    outgoing = dot(sel.astype(BF16), normed)
    for e in range(E):
        disp_send[e] = outgoing[e * cap : (e + 1) * cap].astype(BF16)
    d_copies = []
    for i, peer in enumerate(expert_peers):
        copy = pltpu.make_async_remote_copy(
            src_ref=disp_send.at[peer],
            dst_ref=disp_recv.at[me_e],
            send_sem=ds_sem.at[i],
            recv_sem=dr_sem.at[i],
            device_id={"expert": peer},
            device_id_type=MESH,
        )
        copy.start()
        d_copies.append(copy)
    disp_recv[me_e] = disp_send[me_e]
    copies[3].wait()
    copies[4].wait()
    copies[5].wait()
    for copy in d_copies:
        copy.wait()
    arrived = jnp.concatenate([disp_recv[e].astype(F32) for e in range(E)], axis=0).astype(BF16)

    gate = dot_nt(arrived, gbuf[...])
    upward = dot_nt(arrived, ubuf[...])
    active = (gate * jax.nn.sigmoid(GLU_SLOPE * gate) * (upward + 1.0)).astype(BF16)
    expert_part = dot(active, dbuf[...])

    for t in range(T):
        part_send[t] = expert_part[:, t * slab : (t + 1) * slab].astype(BF16)
    p_copies = []
    for i, peer in enumerate(tensor_peers):
        copy = pltpu.make_async_remote_copy(
            src_ref=part_send.at[peer],
            dst_ref=part_recv.at[i],
            send_sem=ps_sem.at[i],
            recv_sem=pr_sem.at[i],
            device_id={"tensor": peer},
            device_id_type=MESH,
        )
        copy.start()
        p_copies.append(copy)
    summed = part_send[me_t].astype(F32)
    for i, copy in enumerate(p_copies):
        copy.wait()
        summed = summed + part_recv[i].astype(F32)

    for e in range(E):
        ret_send[e] = summed[e * cap : (e + 1) * cap].astype(BF16)
    r_copies = []
    for i, peer in enumerate(expert_peers):
        copy = pltpu.make_async_remote_copy(
            src_ref=ret_send.at[peer],
            dst_ref=ret_recv.at[me_e],
            send_sem=rs_sem.at[i],
            recv_sem=rr_sem.at[i],
            device_id={"expert": peer},
            device_id_type=MESH,
        )
        copy.start()
        r_copies.append(copy)
    ret_recv[me_e] = ret_send[me_e]
    kept = res_slab[me_t]
    for copy in r_copies:
        copy.wait()
    returned = jnp.concatenate([ret_recv[e].astype(F32) for e in range(E)], axis=0).astype(BF16)
    blended = dot_tn(mix_hi, returned) + (dot_tn(mix_mid, returned) + dot_tn(mix_lo, returned))
    out_ref[...] = (kept + blended).astype(BF16)


def per_device(
    hidden_in,
    queries,
    new_keys,
    new_values,
    cache_keys,
    cache_values,
    cache_lengths,
    out_weight,
    norm_gain,
    expert_ids,
    route_probs,
    route_order,
    gate_weight,
    up_weight,
    down_weight,
):
    S, D = hidden_in.shape
    E = lax.axis_size("expert")
    T = lax.axis_size("tensor")
    assert gate_weight.shape[0] == 1
    H, HD = queries.shape[1:]
    G = new_keys.shape[1]
    C = cache_keys.shape[3]
    F = gate_weight.shape[2]
    top = expert_ids.shape[1]
    cap = min(S, max(2, (S * top + E - 1) // E))
    slab = D // T
    chunks = widths_of(D)
    sizes = (S, H, G, HD, C, D, F, E, T, cap)
    vmem = pl.BlockSpec(memory_space=pltpu.VMEM)
    hbm = pl.BlockSpec(memory_space=pl.ANY)
    smem = pl.BlockSpec(memory_space=pltpu.SMEM)
    scratch = [
        pltpu.VMEM(cache_keys.shape, BF16),
        pltpu.VMEM(cache_values.shape, BF16),
        pltpu.VMEM((D, H * HD), BF16),
        pltpu.VMEM((F, D), BF16),
        pltpu.VMEM((F, D), BF16),
        pltpu.VMEM((F, D), BF16),
        pltpu.VMEM((T, S, slab), F32),
        pltpu.VMEM((E, cap, D), BF16),
        pltpu.VMEM((E, cap, D), BF16),
        pltpu.VMEM((T, E * cap, slab), BF16),
        pltpu.VMEM((T - 1, E * cap, slab), BF16),
        pltpu.VMEM((E, cap, slab), BF16),
        pltpu.VMEM((E, cap, slab), BF16),
        pltpu.SemaphoreType.DMA((6,)),
        pltpu.SemaphoreType.DMA((len(chunks), T - 1)),
        pltpu.SemaphoreType.DMA((len(chunks), T - 1)),
        pltpu.SemaphoreType.DMA((E - 1,)),
        pltpu.SemaphoreType.DMA((E - 1,)),
        pltpu.SemaphoreType.DMA((T - 1,)),
        pltpu.SemaphoreType.DMA((T - 1,)),
        pltpu.SemaphoreType.DMA((E - 1,)),
        pltpu.SemaphoreType.DMA((E - 1,)),
    ]
    scratch += [pltpu.VMEM((S, n), BF16) for _, n in chunks]
    scratch += [pltpu.VMEM((T - 1, S, n), BF16) for _, n in chunks]
    return pl.pallas_call(
        functools.partial(kernel, sizes),
        out_shape=jax.ShapeDtypeStruct((S, slab), BF16),
        in_specs=[smem] + [vmem] * 8 + [hbm] * 6,
        out_specs=vmem,
        scratch_shapes=scratch,
        compiler_params=pltpu.CompilerParams(
            collective_id=0, has_side_effects=True, vmem_limit_bytes=60 * 1024 * 1024
        ),
    )(
        cache_lengths,
        hidden_in,
        queries,
        new_keys,
        new_values,
        norm_gain,
        expert_ids.T,
        route_probs.T,
        route_order.T,
        cache_keys,
        cache_values,
        out_weight.T,
        gate_weight.transpose(0, 2, 1),
        up_weight.transpose(0, 2, 1),
        down_weight,
    )


def solution(mesh):
    in_specs = (
        P(("groups", "expert"), None),
        P(("groups", "expert"), "tensor", None),
        P(("groups", "expert"), "tensor", None),
        P(("groups", "expert"), "tensor", None),
        P(("groups", "expert"), "tensor", None, None),
        P(("groups", "expert"), "tensor", None, None),
        P(("groups", "expert")),
        P("tensor", None),
        P(),
        P(("groups", "expert"), None),
        P(("groups", "expert"), None),
        P(("groups", "expert"), None),
        P("expert", None, "tensor"),
        P("expert", None, "tensor"),
        P("expert", "tensor", None),
    )
    out_specs = P(("groups", "expert"), "tensor")
    return jax.shard_map(
        per_device, mesh=mesh, in_specs=in_specs, out_specs=out_specs, check_vma=False
    )
```

time: 104 us -> 30.4 us (0.29)
  waiting for transfers between devices: 38.3 us -> 0 us
  Pallas kernels: 0 us -> 28.9 us
  blocking collectives: 27.1 us -> 0 us
  matrix products: 17.2 us -> 0 us
  between operations: 13.6 us -> 0.01 us
  other arithmetic: 3.95 us -> 0 us
  local copies, waits for them, and re-layouts: 2.93 us -> 1.35 us
    pallas_call x0 -> x1, Pallas kernels: none -> 28.9 us  [per_device(): pl.pallas_call(functools.partial(kernel, sizes), out_shape=jax.ShapeDtype...]
    all_to_all x2 -> x0, blocking collectives: 27.1 us -> none  [the longest x1 14.5 us: per_device(): lax.all_to_all(expert_part, 'expert', split_axis=0, concat_axis=0, tiled=...]
    psum x1 -> x0, waiting for transfers between devices: 23.1 us -> none  [per_device(): attention = lax.psum(partial_sums, 'tensor')]
    dot_general x9 -> x0, matrix products: 17.2 us -> none  [the longest x1 4.97 us: per_device(): jnp.dot(attended, out_weight, preferred_element_type=jnp.float32)]
    unnamed x3 -> x0, waiting for transfers between devices: 15.1 us -> none
    reduce_sum x5 -> x0, other arithmetic: 1.54 us -> none  [the longest x1 1.03 us: apply_norm(): mean_square = jnp.mean(residual * residual, axis=1, keepdims=True)]
    convert_element_type x4 -> x0, other arithmetic: 1.51 us -> none  [the longest x1 0.71 us: per_device(): return (kept + expert_mixture).astype(jnp.bfloat16)]
    unnamed x19 -> x1, local copies, waits for them, and re-layouts: 2.39 us -> 1.35 us
  transfers between devices with their start and end apart: 2 -> 0, of which waited for: 2 -> 0; matrix products, arithmetic and copies ran while one was open for 1% -> 0% of each run, Pallas kernels for 0% -> 0%
where the time goes in v1:
time: 30.4 us; the launch traced here: 30.2 us
  Pallas kernels  28.9 us (95%)
  local copies, waits for them, and re-layouts  1.35 us (4%)
    pallas_call x1, Pallas kernels, per_device(): pl.pallas_call(functools.partial(kernel, sizes), out_shape=jax.ShapeDtype...  28.9 us
    unnamed x1, local copies, waits for them, and re-layouts  1.35 us

profile of v1, /device:TPU:0, one launch (start us, length us, event | category | flops | bytes accessed | tf_op | source)
XLA Modules:
  0.0 30.2 jit_solution(13668957882016381976)
XLA Ops:
  0.0 28.9 %shard_map.145 = bf16[8,1440]{1,0:T(8,128)(2,1)} custom-call(s32[8]{0:T(128)} %len_ref.1, bf16[8,2880]{1,0:T(8,128)(2,1)} %hid_ref.1, bf16[8,16,64]{2,1,0:T(8,128)(2,1)} %q_ref.1, bf16[8,4,64]{2,1,0:T(4,128)(2,1)} %nk_ref.1, bf16[8,4,64]{2,1,0:T(4,128)(2,1)} %nv_ref.1, f32[2880]{0:T(1024)} %gain_ref.1, s32[4,8]{1,0:T(4,128)} %bitcast.9, f32[4,8]{1,0:T(4,128)} %bitcast.10, ...), custom_call_target="tpu_custom_call" | custom-call | tf_op jit(solution)/shard_map/pallas_call | solution.py:348
  28.9 1.3 %copy.17 = bf16[8,1440]{1,0:T(8,128)(2,1)} copy(bf16[8,1440]{1,0:T(8,128)(2,1)} %shard_map.145) | data formatting | bytes 46080

commit v2 on v1

v2 whole, which is shorter than its diff:
```python
import functools

import jax
import jax.numpy as jnp
from jax import lax
from jax.experimental import pallas as pl
from jax.experimental.pallas import tpu as pltpu
from jax.sharding import PartitionSpec as P

EPSILON = 1e-05
GLU_SLOPE = 1.702
MESH = pl.DeviceIdType.MESH
BF16 = jnp.bfloat16
F32 = jnp.float32
CHUNK = 1024
PART = 1536
LANES = 128


def dot(a, b):
    return jnp.dot(a, b, preferred_element_type=F32)


def dot_nt(a, b):
    return lax.dot_general(a, b, (((1,), (1,)), ((), ())), preferred_element_type=F32)


def dot_tn(a, b):
    return lax.dot_general(a, b, (((0,), (0,)), ((), ())), preferred_element_type=F32)


def widths_of(total, step):
    return [(start, min(step, total - start)) for start in range(0, total, step)]


def split_three(x):
    high = x.astype(BF16)
    rest = x - high.astype(F32)
    middle = rest.astype(BF16)
    low = (rest - middle.astype(F32)).astype(BF16)
    return high, middle, low


def kernel(
    sizes,
    len_ref,
    hid_ref,
    q_ref,
    nk_ref,
    nv_ref,
    gain_ref,
    ids_ref,
    probs_ref,
    order_ref,
    k_hbm,
    v_hbm,
    w_hbm,
    gate_hbm,
    up_hbm,
    down_hbm,
    out_ref,
    kbuf,
    vbuf,
    wbuf,
    gbuf,
    ubuf,
    dbuf,
    res_slab,
    local_sem,
    weight_sem,
    xs_sem,
    xr_sem,
    ds_sem,
    dr_sem,
    rs_sem,
    rr_sem,
    *bufs,
):
    S, H, G, HD, C, D, F, E, T, cap = sizes
    R = H // G
    slab = D // T
    chunks = widths_of(D, CHUNK)
    parts = widths_of(slab, PART)
    groups = []
    taken = 0
    for count in [len(chunks)] * 4 + [len(parts)] * 2:
        groups.append(bufs[taken : taken + count])
        taken += count
    x_send, x_recv, disp_send, disp_recv, ret_send, ret_recv = groups
    me_e = lax.axis_index("expert")
    me_t = lax.axis_index("tensor")

    k_copy = pltpu.make_async_copy(k_hbm, kbuf, local_sem.at[0])
    v_copy = pltpu.make_async_copy(v_hbm, vbuf, local_sem.at[1])
    w_copies = [
        pltpu.make_async_copy(w_hbm.at[pl.ds(a, n)], wbuf.at[pl.ds(a, n)], weight_sem.at[c])
        for c, (a, n) in enumerate(chunks)
    ]
    gate_copy = pltpu.make_async_copy(gate_hbm.at[0], gbuf, local_sem.at[2])
    up_copy = pltpu.make_async_copy(up_hbm.at[0], ubuf, local_sem.at[3])
    down_copy = pltpu.make_async_copy(down_hbm.at[0], dbuf, local_sem.at[4])
    k_copy.start()
    v_copy.start()
    for copy in w_copies:
        copy.start()

    barrier = pltpu.get_barrier_semaphore()
    tensor_peers = [lax.rem(me_t + i, T) for i in range(1, T)]
    expert_peers = [lax.rem(me_e + i, E) for i in range(1, E)]
    peers = [
        {"expert": lax.rem(me_e + i, E), "tensor": lax.rem(me_t + j, T)}
        for i in range(E)
        for j in range(T)
        if i + j > 0
    ]
    for peer in peers:
        pl.semaphore_signal(barrier, inc=1, device_id=peer, device_id_type=MESH)

    ids = ids_ref[...]
    probs = probs_ref[...]
    order = order_ref[...]
    top = ids.shape[0]
    slots = E * cap
    row = lax.broadcasted_iota(jnp.int32, (slots, S), 0)
    slot_expert = row // cap
    slot_place = (row % cap).astype(F32)
    picked = jnp.zeros((top, S), F32)
    for j in range(top):
        picked = picked + jnp.where(order == j, probs[j : j + 1], 0.0)
    weights = picked / jnp.sum(probs, axis=0, keepdims=True)
    member = jnp.zeros((slots, S), F32)
    mixture = jnp.zeros((slots, S), F32)
    for j in range(top):
        hit = ids[j : j + 1] == slot_expert
        member = member + jnp.where(hit, 1.0, 0.0)
        mixture = mixture + jnp.where(hit, weights[j : j + 1], 0.0)
    earlier = jnp.where(
        lax.broadcasted_iota(jnp.int32, (S, S), 0) < lax.broadcasted_iota(jnp.int32, (S, S), 1),
        1.0,
        0.0,
    )
    place = dot(member.astype(BF16), earlier.astype(BF16))
    sel = jnp.where(place == slot_place, member, 0.0)
    mixture = mixture * sel
    mixture = split_three(mixture)
    sel = sel.astype(BF16)

    scaling = 1.0 / HD**0.5
    width = G * HD
    diagonal = (lax.broadcasted_iota(jnp.int32, (H, width), 0) // R) == (
        lax.broadcasted_iota(jnp.int32, (H, width), 1) // HD
    )
    position = lax.broadcasted_iota(jnp.int32, (H, C), 1)
    k_copy.wait()
    scores, owns = [], []
    for s in range(S):
        wide = jnp.concatenate([q_ref[s].astype(F32)] * G, axis=1)
        wide = jnp.where(diagonal, wide, 0.0)
        raw = dot(wide.astype(BF16), kbuf[s].reshape(width, C)) * scaling
        scores.append(jnp.where(position < len_ref[s], raw, -1e30))
        new_key = nk_ref[s].astype(F32)
        row = jnp.concatenate([new_key[g : g + 1] for g in range(G)], axis=1)
        owns.append(jnp.sum(wide * row, axis=1, keepdims=True) * scaling)
    score = jnp.concatenate(scores, axis=0)
    own = jnp.concatenate(owns, axis=0)
    highest = jnp.maximum(jnp.max(score, axis=1, keepdims=True), own)
    grown = jnp.exp(score - highest)
    own_grown = jnp.exp(own - highest)
    total = jnp.sum(grown, axis=1, keepdims=True) + own_grown
    prob = (grown / total).astype(BF16)
    own_prob = (own_grown / total).astype(BF16).astype(F32)
    v_copy.wait()
    attended = []
    for s in range(S):
        rows = slice(s * H, (s + 1) * H)
        mixed = dot_nt(prob[rows], vbuf[s].reshape(width, C))
        new_value = nv_ref[s].astype(F32)
        row = jnp.concatenate([new_value[g : g + 1] for g in range(G)], axis=1)
        attended.append(jnp.where(diagonal, mixed + own_prob[rows] * row, 0.0))
    attended = jnp.concatenate(attended, axis=0).astype(BF16)
    out_row = lax.broadcasted_iota(jnp.int32, (R * S, S * H), 0)
    in_row = lax.broadcasted_iota(jnp.int32, (R * S, S * H), 1)
    regroup = jnp.where(
        ((out_row % S) == (in_row // H)) & ((out_row // S) == (in_row % R)), 1.0, 0.0
    ).astype(BF16)
    grouped = dot(regroup, attended)
    heads = jnp.concatenate(
        [
            grouped[r * S : (r + 1) * S, g * HD : (g + 1) * HD]
            for g in range(G)
            for r in range(R)
        ],
        axis=1,
    ).astype(BF16)

    pl.semaphore_wait(barrier, len(peers))
    residuals, x_copies = [], []
    for c, (a, n) in enumerate(chunks):
        w_copies[c].wait()
        if c == len(chunks) - 1:
            gate_copy.start()
            up_copy.start()
            down_copy.start()
        partial = dot_nt(heads, wbuf[a : a + n])
        x_send[c][...] = partial.astype(BF16)
        x_copies.append([])
        for i, peer in enumerate(tensor_peers):
            copy = pltpu.make_async_remote_copy(
                src_ref=x_send[c],
                dst_ref=x_recv[c].at[i],
                send_sem=xs_sem.at[c, i],
                recv_sem=xr_sem.at[c, i],
                device_id={"tensor": peer},
                device_id_type=MESH,
            )
            copy.start()
            x_copies[c].append(copy)
        residuals.append(hid_ref[:, a : a + n].astype(F32) + partial)

    gain = gain_ref[...].reshape(1, D)
    square = jnp.zeros((S, 1), F32)
    d_copies = []
    for c, (a, n) in enumerate(chunks):
        for i, copy in enumerate(x_copies[c]):
            copy.wait()
            residuals[c] = residuals[c] + x_recv[c][i].astype(F32)
        square = square + jnp.sum(residuals[c] * residuals[c], axis=1, keepdims=True)
        rows = (residuals[c] * gain[:, a : a + n]).astype(BF16)
        if c == len(chunks) - 1:
            factor = lax.rsqrt(square * (1.0 / D) + EPSILON)
            lane = lax.broadcasted_iota(jnp.int32, (S, LANES), 1)
            extra = jnp.zeros((S, LANES), F32)
            for i, term in enumerate(split_three(factor)):
                extra = jnp.where(lane == i, term.astype(F32), extra)
            rows = jnp.concatenate([extra.astype(BF16), rows], axis=1)
        outgoing = dot(sel, rows)
        for e in range(E):
            disp_send[c][e] = outgoing[e * cap : (e + 1) * cap].astype(BF16)
        d_copies.append([])
        for i, peer in enumerate(expert_peers):
            copy = pltpu.make_async_remote_copy(
                src_ref=disp_send[c].at[peer],
                dst_ref=disp_recv[c].at[me_e],
                send_sem=ds_sem.at[c, i],
                recv_sem=dr_sem.at[c, i],
                device_id={"expert": peer},
                device_id_type=MESH,
            )
            copy.start()
            d_copies[c].append(copy)
        disp_recv[c][me_e] = disp_send[c][me_e]
    residual = jnp.concatenate(residuals, axis=1)
    for t in range(T):
        res_slab[t] = residual[:, t * slab : (t + 1) * slab]

    gate_copy.wait()
    up_copy.wait()
    gate = jnp.zeros((slots, F), F32)
    upward = jnp.zeros((slots, F), F32)
    for c, (a, n) in enumerate(chunks):
        for copy in d_copies[c]:
            copy.wait()
        arrived = jnp.concatenate([disp_recv[c][e].astype(F32) for e in range(E)], axis=0)
        if c == len(chunks) - 1:
            factor = jnp.sum(arrived[:, :LANES], axis=1, keepdims=True)
            arrived = arrived[:, LANES:]
        arrived = arrived.astype(BF16)
        gate = gate + dot_nt(arrived, gbuf[:, a : a + n])
        upward = upward + dot_nt(arrived, ubuf[:, a : a + n])
    gate = gate * factor
    upward = upward * factor
    active = (gate * jax.nn.sigmoid(GLU_SLOPE * gate) * (upward + 1.0)).astype(BF16)

    down_copy.wait()
    r_copies = []
    for c, (a, n) in enumerate(parts):
        for t in range(T):
            first = t * slab + a
            low = first // LANES * LANES
            high = min(D, -(-(first + n) // LANES) * LANES)
            product = dot(active, dbuf[:, low:high])[:, first - low : first - low + n]
            for e in range(E):
                ret_send[c][t, e] = product[e * cap : (e + 1) * cap].astype(BF16)
        r_copies.append([])
        for i, peer in enumerate(peers):
            copy = pltpu.make_async_remote_copy(
                src_ref=ret_send[c].at[peer["tensor"], peer["expert"]],
                dst_ref=ret_recv[c].at[me_t, me_e],
                send_sem=rs_sem.at[c, i],
                recv_sem=rr_sem.at[c, i],
                device_id=peer,
                device_id_type=MESH,
            )
            copy.start()
            r_copies[c].append(copy)
        ret_recv[c][me_t, me_e] = ret_send[c][me_t, me_e]

    kept = res_slab[me_t]
    for c, (a, n) in enumerate(parts):
        for copy in r_copies[c]:
            copy.wait()
        returned = jnp.zeros((slots, n), F32)
        for t in range(T):
            returned = returned + jnp.concatenate(
                [ret_recv[c][t, e].astype(F32) for e in range(E)], axis=0
            )
        high, middle, low = split_three(returned)
        blended = dot_tn(mixture[0], high)
        blended = blended + (dot_tn(mixture[1], high) + dot_tn(mixture[0], middle))
        blended = blended + (
            dot_tn(mixture[2], high) + dot_tn(mixture[1], middle) + dot_tn(mixture[0], low)
        )
        out_ref[:, a : a + n] = (kept[:, a : a + n] + blended).astype(BF16)


def per_device(
    hidden_in,
    queries,
    new_keys,
    new_values,
    cache_keys,
    cache_values,
    cache_lengths,
    out_weight,
    norm_gain,
    expert_ids,
    route_probs,
    route_order,
    gate_weight,
    up_weight,
    down_weight,
):
    S, D = hidden_in.shape
    E = lax.axis_size("expert")
    T = lax.axis_size("tensor")
    assert gate_weight.shape[0] == 1
    H, HD = queries.shape[1:]
    G = new_keys.shape[1]
    C = cache_keys.shape[3]
    F = gate_weight.shape[2]
    top = expert_ids.shape[1]
    cap = min(S, max(2, (S * top + E - 1) // E))
    slab = D // T
    chunks = widths_of(D, CHUNK)
    parts = widths_of(slab, PART)
    sizes = (S, H, G, HD, C, D, F, E, T, cap)
    vmem = pl.BlockSpec(memory_space=pltpu.VMEM)
    hbm = pl.BlockSpec(memory_space=pl.ANY)
    smem = pl.BlockSpec(memory_space=pltpu.SMEM)
    scratch = [
        pltpu.VMEM(cache_keys.shape, BF16),
        pltpu.VMEM(cache_values.shape, BF16),
        pltpu.VMEM((D, H * HD), BF16),
        pltpu.VMEM((F, D), BF16),
        pltpu.VMEM((F, D), BF16),
        pltpu.VMEM((F, D), BF16),
        pltpu.VMEM((T, S, slab), F32),
        pltpu.SemaphoreType.DMA((5,)),
        pltpu.SemaphoreType.DMA((len(chunks),)),
        pltpu.SemaphoreType.DMA((len(chunks), T - 1)),
        pltpu.SemaphoreType.DMA((len(chunks), T - 1)),
        pltpu.SemaphoreType.DMA((len(chunks), E - 1)),
        pltpu.SemaphoreType.DMA((len(chunks), E - 1)),
        pltpu.SemaphoreType.DMA((len(parts), T * E - 1)),
        pltpu.SemaphoreType.DMA((len(parts), T * E - 1)),
    ]
    wide = [n for _, n in chunks]
    sent = wide[:-1] + [wide[-1] + LANES]
    narrow = [n for _, n in parts]
    scratch += [pltpu.VMEM((S, n), BF16) for n in wide]
    scratch += [pltpu.VMEM((T - 1, S, n), BF16) for n in wide]
    scratch += [pltpu.VMEM((E, cap, n), BF16) for n in sent] * 2
    scratch += [pltpu.VMEM((T, E, cap, n), BF16) for n in narrow] * 2
    return pl.pallas_call(
        functools.partial(kernel, sizes),
        out_shape=jax.ShapeDtypeStruct((S, slab), BF16),
        in_specs=[smem] + [vmem] * 8 + [hbm] * 6,
        out_specs=vmem,
        scratch_shapes=scratch,
        compiler_params=pltpu.CompilerParams(
            collective_id=0, has_side_effects=True, vmem_limit_bytes=60 * 1024 * 1024
        ),
    )(
        cache_lengths,
        hidden_in,
        queries,
        new_keys,
        new_values,
        norm_gain,
        expert_ids.T,
        route_probs.T,
        route_order.T,
        cache_keys,
        cache_values,
        out_weight.T,
        gate_weight.transpose(0, 2, 1),
        up_weight.transpose(0, 2, 1),
        down_weight,
    )


def solution(mesh):
    in_specs = (
        P(("groups", "expert"), None),
        P(("groups", "expert"), "tensor", None),
        P(("groups", "expert"), "tensor", None),
        P(("groups", "expert"), "tensor", None),
        P(("groups", "expert"), "tensor", None, None),
        P(("groups", "expert"), "tensor", None, None),
        P(("groups", "expert")),
        P("tensor", None),
        P(),
        P(("groups", "expert"), None),
        P(("groups", "expert"), None),
        P(("groups", "expert"), None),
        P("expert", None, "tensor"),
        P("expert", None, "tensor"),
        P("expert", "tensor", None),
    )
    out_specs = P(("groups", "expert"), "tensor")
    return jax.shard_map(
        per_device, mesh=mesh, in_specs=in_specs, out_specs=out_specs, check_vma=False
    )
```

time: 30.4 us -> 27.6 us (0.908)
  the two profiles are of different devices: /device:TPU:0 before, /device:TPU:1 now
where the time goes in v2:
time: 27.6 us; the launch traced here: 27.4 us
  Pallas kernels  26 us (94%)
  local copies, waits for them, and re-layouts  1.35 us (5%)
    pallas_call x1, Pallas kernels, per_device(): pl.pallas_call(functools.partial(kernel, sizes), out_shape=jax.ShapeDtype...  26 us
    unnamed x1, local copies, waits for them, and re-layouts  1.35 us

profile of v2, /device:TPU:1, one launch (start us, length us, event | category | flops | bytes accessed | tf_op | source)
XLA Modules:
  0.0 27.4 jit_solution(7436290459432892166)
XLA Ops:
  0.0 26.0 %shard_map.145 = bf16[8,1440]{1,0:T(8,128)(2,1)} custom-call(s32[8]{0:T(128)} %len_ref.1, bf16[8,2880]{1,0:T(8,128)(2,1)} %hid_ref.1, bf16[8,16,64]{2,1,0:T(8,128)(2,1)} %q_ref.1, bf16[8,4,64]{2,1,0:T(4,128)(2,1)} %nk_ref.1, bf16[8,4,64]{2,1,0:T(4,128)(2,1)} %nv_ref.1, f32[2880]{0:T(1024)} %gain_ref.1, s32[4,8]{1,0:T(4,128)} %bitcast.9, f32[4,8]{1,0:T(4,128)} %bitcast.10, ...), custom_call_target="tpu_custom_call" | custom-call | tf_op jit(solution)/shard_map/pallas_call | solution.py:374
  26.1 1.3 %copy.17 = bf16[8,1440]{1,0:T(8,128)(2,1)} copy(bf16[8,1440]{1,0:T(8,128)(2,1)} %shard_map.145) | data formatting | bytes 46080
